TPU v7x, 32 devices: a whole 2x2x4 slice. The times are simulated.
32 devices in a mesh: rows: 32 (over z, y, x, core).
Axes of the slice: x: 2, y: 2, z: 4, core: 2. Of those that a mesh axis runs over, the one named last changes fastest.
Arguments:
- source: float32 [64, 131072], P(None, 'rows'), may hold values from -6 to 6
- band_values: float32 [128, 131072], P(None, 'rows'), may hold values from -0.625 to 0.625
- offsets: int32 [128], replicated, may hold values from -128 to 128, as said below
Outputs:
- compressed: float32 [128, 131072], P(None, 'rows')
Inputs may be any that keep to these rules, and one draw needn't show every extreme that they name: The 128 offsets are distinct and include both -128 and 128.
All inputs are finite; a program needn't handle non-finite values.
Results may differ from a plain program's by a relative error of at most 0.0003.
Values sent between devices are 32-bit elements; how exact they have to be, the bound alone decides.
A program may use at most 192 MiB of HBM per device.

v0:
```python
import jax
import jax.numpy as jnp
from jax import lax
from jax.sharding import PartitionSpec as P

HB = 128
K2 = 128


def padded(block, sides, width):
    for axis, dim in sides:
        count = lax.axis_size(axis)
        forward = [(i, i + 1) for i in range(count - 1)]
        backward = [(target, source) for source, target in forward]
        low = lax.ppermute(
            lax.slice_in_dim(block, block.shape[dim] - width, None, axis=dim), axis, forward
        )
        high = lax.ppermute(lax.slice_in_dim(block, 0, width, axis=dim), axis, backward)
        block = jnp.concatenate([low, block, high], axis=dim)
    return block


def band_blocks(band_values, offsets):
    diagonals = band_values.shape[0]
    blocks = band_values.shape[1] // HB
    values = band_values.reshape(diagonals, blocks, HB).transpose(1, 0, 2)
    within = jnp.arange(HB, dtype=jnp.int32)
    columns = within[None, :] + offsets[:, None] + HB
    row_index = jnp.broadcast_to(within[None, :], columns.shape)
    blocked = jnp.zeros((blocks, HB, 3 * HB), values.dtype)
    return blocked.at[:, row_index, columns].set(values)


def apply_band(extended, blocked):
    width = extended.shape[0]
    blocks = blocked.shape[0]
    pieces = extended.reshape(width, blocks + 2, HB)
    windows = jnp.concatenate([pieces[:, :-2], pieces[:, 1:-1], pieces[:, 2:]], axis=2)
    result = jnp.einsum("cbj,brj->cbr", windows, blocked, precision=lax.Precision.HIGHEST)
    return result.reshape(width, blocks * HB)


def compress(grammian, retain):
    spanning = grammian[:, :retain]
    coeffs = None
    for repeat in range(2):
        if repeat > 0:
            spanning = jnp.dot(grammian, coeffs.T, precision=lax.Precision.HIGHEST)
        mapped = jnp.dot(grammian, spanning, precision=lax.Precision.HIGHEST)
        metric = jnp.dot(spanning.T, mapped, precision=lax.Precision.HIGHEST)
        metric = 0.5 * (metric + metric.T)
        factor = jnp.linalg.cholesky(metric)
        coeffs = jax.scipy.linalg.solve_triangular(factor, spanning.T, lower=True)
    return coeffs


def gram_total(stacked, total):
    local = jnp.dot(stacked, stacked.T, precision=lax.Precision.HIGHEST)
    summed = lax.psum(local, "rows")
    return summed / total


def first_gram(first, total):
    return gram_total(first, total)


def second_gram(factor, squared, total):
    return gram_total(jnp.concatenate([factor, squared], axis=0), total)


def body(source, band_values, offsets):
    devices_here = lax.axis_size("rows")
    total = float(source.shape[1] * devices_here)
    keep_first = 2 * source.shape[0]
    deep_source = padded(source, (("rows", 1),), 3 * HB)
    deep_band = padded(band_values, (("rows", 1),), 2 * HB)
    blocked = band_blocks(deep_band, offsets)
    first_deep = jnp.concatenate([deep_source[:, HB:-HB], apply_band(deep_source, blocked)], axis=0)
    first = first_deep[:, 2 * HB : -2 * HB]
    gram_one = first_gram(first, total)
    coeffs_one = compress(gram_one, keep_first)
    factor_deep = jnp.dot(coeffs_one, first_deep, precision=lax.Precision.HIGHEST)
    factor = factor_deep[:, 2 * HB : -2 * HB]
    once_more = apply_band(factor_deep, blocked[1:-1])
    squared = apply_band(once_more, blocked[2:-2])
    second = jnp.concatenate([factor, squared], axis=0)
    coeffs_two = compress(second_gram(factor, squared, total), K2)
    return jnp.dot(coeffs_two, second, precision=lax.Precision.HIGHEST)


def solution(mesh):
    placed = (P(None, "rows"), P(None, "rows"), P())
    return jax.shard_map(
        body, mesh=mesh, in_specs=placed, out_specs=P(None, "rows"), check_vma=False
    )
```

profile of v0, /device:TPU:0, one launch (start us, length us, event | category | flops | bytes accessed | tf_op | source)
XLA Modules:
  0.0 541.9 jit_solution(10150455950687637669)
XLA Ops:
  10.6 3.7 collective-permute-start.2
  14.3 3.9 collective-permute-start
  29.6 2.5 pad_maximum_fusion.3
  32.0 8.6 %copy.98 = f32[128,128,36]{2,1,0:T(8,128)} copy(f32[128,128,36]{0,1,2:T(8,128)} %bitcast.109) | data formatting | bytes 4718592 | tf_op jit(solution)/shard_map/transpose | solution.py:26
  40.6 51.0 %scatter_custom_fusion = f32[36,49152]{0,1:T(8,128)} fusion(s32[16384]{0:T(1024)} %select_bitcast_fusion, f32[16384,36]{1,0:T(8,128)} %bitcast.111, f32[]{:T(128)} %constant.47.clone.1), kind=kCustom, calls=%fused_computation.1 | custom fusion | bytes 7078400
  91.7 17.8 %copy.79 = f32[36,128,384]{2,1,0:T(8,128)} copy(f32[36,128,384]{0,2,1:T(8,128)} %bitcast.101) | data formatting | bytes 14155776 | tf_op jit(solution)/shard_map/scatter | solution.py:31
  109.5 12.0 %fusion.33 = f32[36,8,8,128]{3,2,1,0:T(8,128)S(1)} fusion(f32[36,128,384]{2,1,0:T(8,128)} %copy.79, f32[64,36,128]{2,0,1:T(8,128)S(1)} %copy-done.2, f32[64,36,128]{2,0,1:T(8,128)S(1)} %copy-done.3, f32[64,36,128]{2,0,1:T(8,128)} %copy.103), kind=kOutput, calls=%fused_computation.34 | convolution fusion | flops 1360723968 | bytes 11796480 | tf_op jit(solution)/shard_map/cbj,brj->cbr/dot_general | solution.py:39
  121.5 2.4 fusion.26
  124.0 18.9 %slice.97 = f32[32,49152]{0,1:T(8,128)} slice(f32[36,49152]{0,1:T(8,128)} %scatter_custom_fusion), slice={[2:34], [0:49152]} | slice | bytes 12582912 | tf_op jit(solution)/shard_map/slice | solution.py:85
  143.0 19.0 %slice.98 = f32[34,49152]{0,1:T(8,128)} slice(f32[36,49152]{0,1:T(8,128)} %scatter_custom_fusion), slice={[1:35], [0:49152]} | slice | bytes 13369344 | tf_op jit(solution)/shard_map/slice | solution.py:84
  162.0 17.2 %copy.99 = f32[32,128,384]{2,1,0:T(8,128)} copy(f32[32,128,384]{0,2,1:T(8,128)} %bitcast.103) | data formatting | bytes 12582912 | tf_op jit(solution)/shard_map/slice | solution.py:85
  179.2 17.7 %copy.100 = f32[34,128,384]{2,1,0:T(8,128)} copy(f32[34,128,384]{0,2,1:T(8,128)} %bitcast.102) | data formatting | bytes 13369344 | tf_op jit(solution)/shard_map/slice | solution.py:84
  196.9 52.0 %all-reduce.3.cloned.1.call-done = f32[128,128]{1,0:T(8,128)} async-done(((f32[128,128]{1,0:T(8,128)}), f32[128,128]{1,0:T(8,128)}) %all-reduce.3.cloned.1.call-update) | async-done | bytes 65552 | tf_op jit(solution)/shard_map/psum | solution.py:59
  251.4 11.7 %cholesky.74 = f32[128,128]{1,0:T(8,128)S(1)} custom-call(f32[128,128]{1,0:T(8,128)S(1)} %fusion.63), custom_call_target="Cholesky" | custom-call | tf_op jit(solution)/shard_map/jit(cholesky)/cholesky | solution.py:52
  264.5 9.8 %custom-call.10 = f32[1,128,128]{1,2,0:T(8,128)S(1)} custom-call(f32[1,128,128]{2,1,0:T(8,128)S(1)} %fusion.45), custom_call_target="InvertDiagBlocksLowerTriangular" | custom-call | tf_op jit(solution)/shard_map/jit(_solve_triangular)/triangular_solve | solution.py:53
  278.1 11.7 %cholesky.85 = f32[128,128]{1,0:T(8,128)S(1)} custom-call(f32[128,128]{1,0:T(8,128)S(1)} %fusion.58), custom_call_target="Cholesky" | custom-call | tf_op jit(solution)/shard_map/jit(cholesky)/cholesky | solution.py:52
  291.2 10.2 %custom-call.11 = f32[1,128,128]{1,2,0:T(8,128)S(1)} custom-call(f32[1,128,128]{2,1,0:T(8,128)S(1)} %fusion.46), custom_call_target="InvertDiagBlocksLowerTriangular" | custom-call | tf_op jit(solution)/shard_map/jit(_solve_triangular)/triangular_solve | solution.py:53
  301.7 3.5 fusion.22
  307.2 3.2 slice.96
  310.4 2.9 fusion.99
  313.3 3.1 copy.108
  318.4 3.2 copy.106
  321.5 11.8 %fusion.30 = f32[128,34,128]{0,2,1:T(8,128)S(1)} fusion(f32[34,128,384]{2,1,0:T(8,128)} %copy.100, f32[128,34,128]{2,0,1:T(8,128)} %copy.108, f32[128,34,128]{2,0,1:T(8,128)} %copy.107, f32[128,34,128]{2,0,1:T(8,128)} %copy.106), kind=kOutput, calls=%fused_computation.33 | convolution fusion | flops 2570256384 | bytes 15597568 | tf_op jit(solution)/shard_map/cbj,brj->cbr/dot_general | solution.py:39
  334.1 7.7 %fusion.8 = f32[32,128,128]{2,1,0:T(8,128)} fusion(f32[32,128,384]{2,1,0:T(8,128)S(1)} %bitcast.106, f32[128,32,128]{0,2,1:T(8,128)S(1)} %get-tuple-element.12, f32[128,32,128]{0,2,1:T(8,128)S(1)} %get-tuple-element.13, f32[128,32,128]{0,2,1:T(8,128)S(1)} %get-tuple-element.11), kind=kOutput, calls=%fused_computation.9 | convolution fusion | flops 2419064832 | bytes 14680064 | tf_op jit(solution)/shard_map/cbj,brj->cbr/dot_general | solution.py:39
  341.9 3.2 copy.101
  345.1 6.5 %fusion.21 = f32[256,256]{1,0:T(8,128)} fusion(f32[128,4096]{1,0:T(8,128)} %copy.101, f32[128,4096]{1,0:T(8,128)S(1)} %copy-done.1), kind=kOutput, calls=%fused_computation.23 | convolution fusion | flops 3222274048 | bytes 4456448 | tf_op jit(solution)/shard_map/dot_general | solution.py:58
  351.6 128.0 %all-reduce.5.cloned.1.call-done = f32[256,256]{1,0:T(8,128)} async-done(((f32[256,256]{1,0:T(8,128)}), f32[256,256]{1,0:T(8,128)}) %all-reduce.5.cloned.1.call-update) | async-done | bytes 262160 | tf_op jit(solution)/shard_map/psum | solution.py:59
  481.6 11.7 %cholesky.96 = f32[128,128]{1,0:T(8,128)S(1)} custom-call(f32[128,128]{1,0:T(8,128)S(1)} %fusion.53), custom_call_target="Cholesky" | custom-call | tf_op jit(solution)/shard_map/jit(cholesky)/cholesky | solution.py:52
  494.7 9.8 %custom-call.12 = f32[1,128,128]{1,2,0:T(8,128)S(1)} custom-call(f32[1,128,128]{2,1,0:T(8,128)S(1)} %fusion.47), custom_call_target="InvertDiagBlocksLowerTriangular" | custom-call | tf_op jit(solution)/shard_map/jit(_solve_triangular)/triangular_solve | solution.py:53
  506.2 11.9 %cholesky.107 = f32[128,128]{1,0:T(8,128)S(1)} custom-call(f32[128,128]{1,0:T(8,128)S(1)} %fusion.50), custom_call_target="Cholesky" | custom-call | tf_op jit(solution)/shard_map/jit(cholesky)/cholesky | solution.py:52
  519.5 9.8 %custom-call.13 = f32[1,128,128]{1,2,0:T(8,128)S(1)} custom-call(f32[1,128,128]{2,1,0:T(8,128)S(1)} %fusion.48), custom_call_target="InvertDiagBlocksLowerTriangular" | custom-call | tf_op jit(solution)/shard_map/jit(_solve_triangular)/triangular_solve | solution.py:53
  529.6 5.2 fusion.20
  (97 shorter events, 36.0 us)
Async XLA Ops:
  6.5 13.0 %copy-start.7 = (s32[2]{0:T(128)S(1)}, s32[2]{0:T(128)}, u32[]{:S(2)}) copy-start(s32[2]{0:T(128)} %constant.56) | copy-start | bytes 28
  6.5 13.2 %copy-start.8 = (s32[2]{0:T(128)S(1)}, s32[2]{0:T(128)}, u32[]{:S(2)}) copy-start(s32[2]{0:T(128)} %constant.53) | copy-start | bytes 28
  6.5 7.7 %copy-start.5 = (f32[64,4096]{1,0:T(8,128)S(1)}, f32[64,4096]{1,0:T(8,128)}, u32[]{:S(2)}) copy-start(f32[64,4096]{1,0:T(8,128)} %param.8) | copy-start | bytes 3145732
  6.5 12.9 %copy-start.6 = (s32[128]{0:T(128)S(1)}, s32[128]{0:T(128)}, u32[]{:S(2)}) copy-start(s32[128]{0:T(128)} %param.10) | copy-start | bytes 1540
  6.5 242.4 %all-reduce.3.cloned.1.call-start = ((), (), s32[]{:S(2)}) async-start(), calls=%async_computation | async-start | bytes 131072 | tf_op jit(solution)/shard_map/psum | solution.py:59
  9.3 20.3 %collective-permute-start.3 = (f32[128,256]{0,1:T(8,128)}, f32[128,256]{0,1:T(8,128)S(1)}, u32[]{:S(2)}, u32[]{:S(2)}) collective-permute-start(f32[128,256]{0,1:T(8,128)} %get-tuple-element.15), channel_id=1, source_target_pairs={{1,0},{2,1},{3,2},{4,3},{5,4},{6,5},{7,6},{8,7},{9,8},{10,9},{11,1... | collective-permute-start | bytes 393224 | tf_op jit(solution)/shard_map/ppermute | solution.py:18
  10.6 19.0 %collective-permute-start.2 = (f32[128,256]{0,1:T(8,128)}, f32[128,256]{0,1:T(8,128)}, u32[]{:S(2)}, u32[]{:S(2)}) collective-permute-start(f32[128,256]{0,1:T(8,128)} %get-tuple-element.14), channel_id=1, source_target_pairs={{0,1},{1,2},{2,3},{3,4},{4,5},{5,6},{6,7},{7,8},{8,9},{9,10},{10,1... | collective-permute-start | bytes 393224 | tf_op jit(solution)/shard_map/ppermute | solution.py:15
  14.3 6.1 %collective-permute-start = (f32[64,384]{1,0:T(8,128)S(1)}, f32[64,384]{1,0:T(8,128)S(1)}, u32[]{:S(2)}, u32[]{:S(2)}) collective-permute-start(f32[64,384]{1,0:T(8,128)S(1)} %get-tuple-element.20), channel_id=1, source_target_pairs={{0,1},{1,2},{2,3},{3,4},{4,5},{5,6},{6,7},{7,8},{8,9},{9,10},{10,1... | collective-permute-start | bytes 294920 | tf_op jit(solution)/shard_map/ppermute | solution.py:15
  18.2 3.9 collective-permute-start.1
  91.7 17.8 %copy-start.2 = (f32[64,36,128]{2,0,1:T(8,128)S(1)}, f32[64,36,128]{2,0,1:T(8,128)}, u32[]{:S(2)}) copy-start(f32[64,36,128]{2,0,1:T(8,128)} %copy.105) | copy-start | bytes 3538948
  91.7 17.8 %copy-start.3 = (f32[64,36,128]{2,0,1:T(8,128)S(1)}, f32[64,36,128]{2,0,1:T(8,128)}, u32[]{:S(2)}) copy-start(f32[64,36,128]{2,0,1:T(8,128)} %copy.104) | copy-start | bytes 3538948
  124.0 355.6 %all-reduce.5.cloned.1.call-start = ((), (), s32[]{:S(2)}) async-start(), calls=%async_computation.1 | async-start | bytes 524288 | tf_op jit(solution)/shard_map/psum | solution.py:59
  313.3 3.1 copy-start
  318.4 15.7 %slice-start = ((s8[6291456]{0:T(1024)(128)(4,1)}), s8[2097152]{0:T(1024)(128)(4,1)S(1)}, s32[]{:S(2)}) async-start(s8[6291456]{0:T(1024)(128)(4,1)} %bitcast.105), calls=%async_computation.2 | async-start | bytes 4194304
  321.5 12.6 %slice-start.1 = ((s8[6291456]{0:T(1024)(128)(4,1)}), s8[4194304]{0:T(1024)(128)(4,1)S(1)}, s32[]{:S(2)}) async-start(s8[6291456]{0:T(1024)(128)(4,1)} %bitcast.105), calls=%async_computation.3 | async-start | bytes 8388608
  341.9 3.2 copy-start.1
  479.6 25.2 %copy-start.4 = (f32[256,256]{1,0:T(8,128)S(1)}, f32[256,256]{1,0:T(8,128)}, u32[]{:S(2)}) copy-start(f32[256,256]{1,0:T(8,128)} %all-reduce.5.cloned.1.call-done) | copy-start | bytes 786436
Sparse Core Ops, SparseCore 0:
  124.1 124.8 all-reduce.2
  351.7 127.8 all-reduce.4
where the time goes:
time: 549 us; the launch traced here: 542 us
  local copies, waits for them, and re-layouts  183 us (33%)
  waiting for transfers between devices  180 us (33%)
  other arithmetic  96.5 us (18%)
  matrix products  57.7 us (11%)
  between operations  14.2 us (3%)
  starting transfers between devices  10.2 us (2%)
    psum x2, waiting for transfers between devices, gram_total(): summed = lax.psum(local, 'rows')  180 us
    unnamed x32, local copies, waits for them, and re-layouts  66.7 us
    another operation x12, other arithmetic, compress(): factor = jnp.linalg.cholesky(metric)  49.7 us
    another operation x8, other arithmetic, compress(): coeffs = jax.scipy.linalg.solve_triangular(factor, spanning.T, lower=True)  42.2 us
    slice x2, local copies, waits for them, and re-layouts, body(): once_more = apply_band(factor_deep, blocked[1:-1])  36.8 us
    slice x2, local copies, waits for them, and re-layouts, body(): squared = apply_band(once_more, blocked[2:-2])  36.1 us
    dot_general x3, matrix products, apply_band(): jnp.einsum('cbj,brj->cbr', windows, blocked, precision=lax.Precision.HIGH...  31.5 us
    scatter x1, local copies, waits for them, and re-layouts, band_blocks(): return blocked.at[:, row_index, columns].set(values)  17.8 us
  transfers between devices with their start and end apart: 6, of which 2 were waited for; matrix products, arithmetic and copies ran while one was open for 15% of the time, Pallas kernels for 0%

commit v1 on v0

v1 whole, which is shorter than its diff:
```python
import functools

import jax
import jax.numpy as jnp
from jax import lax
from jax.experimental import pallas as pl
from jax.experimental.pallas import tpu as pltpu
from jax.sharding import PartitionSpec as P

HB = 128
K2 = 128
SUB = 8
MESH = pl.DeviceIdType.MESH
VMEM = pl.BlockSpec(memory_space=pltpu.VMEM)
ANY = pl.BlockSpec(memory_space=pl.ANY)
NT = (((1,), (1,)), ((), ()))


def exact(a, b, dims=(((1,), (0,)), ((), ()))):
    return lax.dot_general(
        a, b, dims, precision=lax.Precision.HIGHEST, preferred_element_type=jnp.float32
    )


def bf(a, b, dims=(((1,), (0,)), ((), ()))):
    return lax.dot_general(a, b, dims, preferred_element_type=jnp.float32)


def halves(value):
    high = value.astype(jnp.bfloat16)
    low = (value - high.astype(jnp.float32)).astype(jnp.bfloat16)
    return high, low


def halo_kernel(n, source, band, low_s, high_s, low_b, high_b, ls, hs, lb, hb, send, recv):
    me = lax.axis_index("rows")
    right, left = lax.rem(me + 1, n), lax.rem(me + n - 1, n)
    barrier = pltpu.get_barrier_semaphore()
    for neighbour in (left, right):
        pl.semaphore_signal(barrier, inc=1, device_id=(neighbour,), device_id_type=MESH)
    pl.semaphore_wait(barrier, 2)
    local = source.shape[1]
    deep_s, deep_b = ls.shape[1], lb.shape[1]
    moves = (
        (band.at[:, pl.ds(local - deep_b, deep_b)], lb, right),
        (band.at[:, pl.ds(0, deep_b)], hb, left),
        (source.at[:, pl.ds(local - deep_s, deep_s)], ls, right),
        (source.at[:, pl.ds(0, deep_s)], hs, left),
    )
    copies = []
    for index, (src, dst, target) in enumerate(moves):
        copies.append(
            pltpu.make_async_remote_copy(
                src_ref=src,
                dst_ref=dst,
                send_sem=send.at[index],
                recv_sem=recv.at[index],
                device_id=(target,),
                device_id_type=MESH,
            )
        )
    for copy in copies:
        copy.start()
    for copy in copies:
        copy.wait()
    low_b[...] = jnp.where(me > 0, lb[...], 0.0)
    high_b[...] = jnp.where(me < n - 1, hb[...], 0.0)
    low_s[...] = jnp.where(me > 0, ls[...], 0.0)
    high_s[...] = jnp.where(me < n - 1, hs[...], 0.0)


def halos(source, band):
    n = lax.axis_size("rows")
    shapes = [(source.shape[0], 3 * HB)] * 2 + [(band.shape[0], 2 * HB)] * 2
    return pl.pallas_call(
        functools.partial(halo_kernel, n),
        out_shape=[jax.ShapeDtypeStruct(shape, jnp.float32) for shape in shapes],
        in_specs=[ANY] * 2,
        out_specs=[VMEM] * 4,
        scratch_shapes=[pltpu.VMEM(shape, jnp.float32) for shape in shapes]
        + [pltpu.SemaphoreType.DMA((4,)), pltpu.SemaphoreType.DMA((4,))],
        compiler_params=pltpu.CompilerParams(collective_id=0, has_side_effects=True),
    )(source, band)


def total_kernel(n, owners, g, out, got, total, gathered, s1, r1, s2, r2):
    me = lax.axis_index("rows")
    stride = n // owners
    mine = me // stride
    barrier = pltpu.get_barrier_semaphore()

    def greet(k, _):
        pl.semaphore_signal(
            barrier, inc=1, device_id=(lax.rem(me + k, n),), device_id_type=MESH
        )
        return 0

    lax.fori_loop(1, n, greet, 0)
    pl.semaphore_wait(barrier, n - 1)

    def outward(o):
        return pltpu.make_async_remote_copy(
            src_ref=g.at[o],
            dst_ref=got.at[me],
            send_sem=s1.at[o],
            recv_sem=r1.at[me],
            device_id=(o * stride,),
            device_id_type=MESH,
        )

    def inward(other):
        return pltpu.make_async_remote_copy(
            src_ref=g.at[0],
            dst_ref=got.at[other],
            send_sem=s1.at[0],
            recv_sem=r1.at[other],
            device_id=(other,),
            device_id_type=MESH,
        )

    def back(other):
        return pltpu.make_async_remote_copy(
            src_ref=total,
            dst_ref=gathered.at[mine],
            send_sem=s2.at[other],
            recv_sem=r2.at[mine],
            device_id=(other,),
            device_id_type=MESH,
        )

    def spread(o):
        return pltpu.make_async_remote_copy(
            src_ref=total,
            dst_ref=gathered.at[o],
            send_sem=s2.at[0],
            recv_sem=r2.at[o],
            device_id=(o * stride,),
            device_id_type=MESH,
        )

    def send_out(k, _):
        o = lax.rem(mine + k, owners)

        @pl.when(o * stride != me)
        def _():
            outward(o).start()

        return 0

    lax.fori_loop(0, owners, send_out, 0)

    @pl.when(mine * stride == me)
    def _():
        got[me] = g[mine]

        def arrive(k, _):
            inward(lax.rem(me + k, n)).wait_recv()
            return 0

        lax.fori_loop(1, n, arrive, 0)
        summed = jnp.sum(got[...], axis=0)
        total[...] = summed
        gathered[mine] = summed

        def send_back(k, _):
            back(lax.rem(me + k, n)).start()
            return 0

        lax.fori_loop(1, n, send_back, 0)

    def collect(o, _):
        @pl.when(o * stride != me)
        def _():
            spread(o).wait_recv()
            outward(o).wait_send()

        return 0

    lax.fori_loop(0, owners, collect, 0)
    out[...] = gathered[...]

    @pl.when(mine * stride == me)
    def _():
        def sent(k, _):
            back(lax.rem(me + k, n)).wait_send()
            return 0

        lax.fori_loop(1, n, sent, 0)


def all_total(value, ident):
    n = lax.axis_size("rows")
    rows, columns = value.shape
    owners = rows // SUB
    shape = (owners, SUB, columns)
    dma = pltpu.SemaphoreType.DMA
    summed = pl.pallas_call(
        functools.partial(total_kernel, n, owners),
        out_shape=jax.ShapeDtypeStruct(shape, jnp.float32),
        in_specs=[VMEM],
        out_specs=VMEM,
        scratch_shapes=[
            pltpu.VMEM((n, SUB, columns), jnp.float32),
            pltpu.VMEM((SUB, columns), jnp.float32),
            pltpu.VMEM(shape, jnp.float32),
            dma((owners,)),
            dma((n,)),
            dma((n,)),
            dma((owners,)),
        ],
        compiler_params=pltpu.CompilerParams(collective_id=ident, has_side_effects=True),
    )(value.reshape(shape))
    return summed.reshape(rows, columns)


def banded(window_high, window_low, band_high, band_low):
    return (
        bf(window_high, band_high, NT)
        + bf(window_low, band_high, NT)
        + bf(window_high, band_low, NT)
    )


def columns_of(block, count=1):
    return pl.ds(pl.multiple_of(block * HB, HB), count * HB)


def first_kernel(
    source, band, offsets, low_s, high_s, low_b, high_b,
    first, upper, lower, gram, high, low, values
):
    width, local = source.shape
    blocks = upper.shape[0]
    for piece, at in ((low_s, 0), (source, 3 * HB), (high_s, 3 * HB + local)):
        part = piece[...]
        where = pl.ds(at, part.shape[1])
        top, bottom = halves(part)
        high[:, where] = top
        low[:, where] = bottom
    first[:width, pl.ds(0, 2 * HB)] = low_s[:, pl.ds(HB, 2 * HB)]
    first[:width, pl.ds(2 * HB, local)] = source[...]
    first[:width, pl.ds(2 * HB + local, 2 * HB)] = high_s[:, pl.ds(0, 2 * HB)]
    values[:, pl.ds(0, 2 * HB)] = low_b[...]
    values[:, pl.ds(2 * HB, local)] = band[...]
    values[:, pl.ds(2 * HB + local, 2 * HB)] = high_b[...]
    diagonals = band.shape[0]
    places = lax.broadcasted_iota(jnp.int32, (diagonals, 3 * HB), 1)
    chosen = jnp.where(places == offsets[...] + HB, 1.0, 0.0).astype(jnp.bfloat16)
    chosen = jnp.concatenate([chosen, chosen], axis=0)

    def step(block, _):
        top, bottom = halves(values[:, columns_of(block)].T)
        spread = bf(jnp.concatenate([top, bottom], axis=1), chosen)
        sheared = pltpu.roll(spread, 0, 1, stride=1, stride_axis=0)
        band_high, band_low = halves(sheared)
        upper[block] = band_high
        lower[block] = band_low
        window = columns_of(block, 3)
        first[width:, columns_of(block)] = banded(
            high[:, window], low[:, window], band_high, band_low
        )
        return 0

    lax.fori_loop(0, blocks, step, 0, unroll=2)
    inner = first[:, pl.ds(2 * HB, local)]
    gram[...] = exact(inner, inner, NT)


def make_first(source, band, offsets, edges):
    width, local = source.shape
    diagonals = band.shape[0]
    deep = local + 4 * HB
    blocks = deep // HB
    return pl.pallas_call(
        first_kernel,
        out_shape=[
            jax.ShapeDtypeStruct((2 * width, deep), jnp.float32),
            jax.ShapeDtypeStruct((blocks, HB, 3 * HB), jnp.bfloat16),
            jax.ShapeDtypeStruct((blocks, HB, 3 * HB), jnp.bfloat16),
            jax.ShapeDtypeStruct((2 * width, 2 * width), jnp.float32),
        ],
        in_specs=[VMEM] * 7,
        out_specs=[VMEM] * 4,
        scratch_shapes=[
            pltpu.VMEM((width, deep + 2 * HB), jnp.bfloat16),
            pltpu.VMEM((width, deep + 2 * HB), jnp.bfloat16),
            pltpu.VMEM((diagonals, deep), jnp.float32),
        ],
        compiler_params=pltpu.CompilerParams(vmem_limit_bytes=60 << 20),
    )(source, band, offsets.reshape(diagonals, 1), *edges)


def eliminate(metric, right):
    order = metric.shape[0]
    tiles = order // SUB
    s = [metric[SUB * t : SUB * t + SUB] for t in range(tiles)]
    y = [right[SUB * t : SUB * t + SUB] for t in range(tiles)]
    rows = lax.broadcasted_iota(jnp.int32, (SUB, 1), 0)
    for j in range(order):
        t0, r = divmod(j, SUB)
        scale = lax.rsqrt(s[t0][r : r + 1, j : j + 1])
        pivot_s = s[t0][r : r + 1] * scale
        pivot_y = y[t0][r : r + 1] * scale
        for t in range(t0, tiles):
            column = s[t][:, j : j + 1] * scale
            if t == t0:
                column = jnp.where(rows > r, column, 0.0)
                y[t] = jnp.where(rows == r, pivot_y, y[t])
            s[t] = s[t] - column * pivot_s
            y[t] = y[t] - column * pivot_y
    return jnp.concatenate(y, axis=0)


def compress(grammian, retain):
    spanning = grammian[:retain]
    coeffs = None
    for repeat in range(2):
        if repeat > 0:
            spanning = exact(coeffs, grammian)
        metric = exact(exact(spanning, grammian), spanning, NT)
        metric = 0.5 * (metric + metric.T)
        coeffs = eliminate(metric, spanning)
    return coeffs


def second_kernel(
    total, summed, first, upper, lower, factor, squared, corner, gram,
    high, low, once_high, once_low
):
    gram_one = summed[...] * (1.0 / total)
    keep = gram_one.shape[0]
    coeffs = compress(gram_one, keep)
    corner[...] = exact(exact(coeffs, gram_one), coeffs, NT)
    blocks = upper.shape[0]
    local = factor.shape[1]
    width = 4 * HB

    def expand(at, _):
        where = pl.ds(pl.multiple_of(at * width, width), width)
        top, bottom = halves(exact(coeffs, first[:, where]))
        high[:, where] = top
        low[:, where] = bottom
        return 0

    lax.fori_loop(0, first.shape[1] // width, expand, 0)

    def once(block, _):
        window = columns_of(block, 3)
        top, bottom = halves(
            banded(high[:, window], low[:, window], upper[block + 1], lower[block + 1])
        )
        once_high[:, columns_of(block)] = top
        once_low[:, columns_of(block)] = bottom
        return 0

    lax.fori_loop(0, blocks - 2, once, 0, unroll=2)

    def twice(block, _):
        window = columns_of(block, 3)
        squared[:, columns_of(block)] = banded(
            once_high[:, window], once_low[:, window], upper[block + 2], lower[block + 2]
        )
        return 0

    lax.fori_loop(0, blocks - 4, twice, 0, unroll=2)
    middle = pl.ds(2 * HB, local)
    factor[...] = high[:, middle].astype(jnp.float32) + low[:, middle].astype(jnp.float32)
    gram[:keep] = exact(factor[...], squared[...], NT)
    gram[keep:] = exact(squared[...], squared[...], NT)


def make_second(summed, first, upper, lower, total):
    keep, deep = first.shape
    local = deep - 4 * HB
    shape = jax.ShapeDtypeStruct
    return pl.pallas_call(
        functools.partial(second_kernel, total),
        out_shape=[
            shape((keep, local), jnp.float32),
            shape((keep, local), jnp.float32),
            shape((keep, keep), jnp.float32),
            shape((2 * keep, keep), jnp.float32),
        ],
        in_specs=[VMEM] * 4,
        out_specs=[VMEM] * 4,
        scratch_shapes=[
            pltpu.VMEM((keep, deep), jnp.bfloat16),
            pltpu.VMEM((keep, deep), jnp.bfloat16),
            pltpu.VMEM((keep, deep - 2 * HB), jnp.bfloat16),
            pltpu.VMEM((keep, deep - 2 * HB), jnp.bfloat16),
        ],
        compiler_params=pltpu.CompilerParams(vmem_limit_bytes=60 << 20),
    )(summed, first, upper, lower)


def last_kernel(total, summed, corner, factor, squared, out):
    keep = corner.shape[0]
    cross = summed[:keep] * (1.0 / total)
    own = summed[keep:] * (1.0 / total)
    top = jnp.concatenate([corner[...], cross], axis=1)
    bottom = jnp.concatenate([cross.T, own], axis=1)
    coeffs = compress(jnp.concatenate([top, bottom], axis=0), K2)
    width = 4 * HB

    def step(at, _):
        where = pl.ds(pl.multiple_of(at * width, width), width)
        stacked = jnp.concatenate([factor[:, where], squared[:, where]], axis=0)
        out[:, where] = exact(coeffs, stacked)
        return 0

    lax.fori_loop(0, out.shape[1] // width, step, 0)


def make_last(summed, corner, factor, squared, total):
    return pl.pallas_call(
        functools.partial(last_kernel, total),
        out_shape=jax.ShapeDtypeStruct((K2, factor.shape[1]), jnp.float32),
        in_specs=[VMEM] * 4,
        out_specs=VMEM,
        compiler_params=pltpu.CompilerParams(vmem_limit_bytes=60 << 20),
    )(summed, corner, factor, squared)


def body(source, band_values, offsets):
    total = float(source.shape[1] * lax.axis_size("rows"))
    edges = halos(source, band_values)
    first, upper, lower, gram = make_first(source, band_values, offsets, edges)
    summed = all_total(gram, 1)
    factor, squared, corner, gram = make_second(summed, first, upper, lower, total)
    summed = all_total(gram, 2)
    return make_last(summed, corner, factor, squared, total)


def solution(mesh):
    placed = (P(None, "rows"), P(None, "rows"), P())
    return jax.shard_map(
        body, mesh=mesh, in_specs=placed, out_specs=P(None, "rows"), check_vma=False
    )
```

time: 549 us -> 147 us (0.27); the launches traced: 542 us -> 147 us
  local copies, waits for them, and re-layouts: 183 us -> 1.39 us
  waiting for transfers between devices: 180 us -> 0 us
  Pallas kernels: 0 us -> 145 us
  other arithmetic: 96.5 us -> 0 us
  matrix products: 57.7 us -> 0 us
  between operations: 14.2 us -> 0.03 us
  starting transfers between devices: 10.2 us -> 0 us
    psum x2 -> x0, waiting for transfers between devices: 180 us -> none  [gram_total(): summed = lax.psum(local, 'rows')]
    pallas_call x0 -> x6, Pallas kernels: none -> 145 us  [the longest x1 47.9 us: make_second(): pl.pallas_call(functools.partial(second_kernel, total), out_shape=[shape(...]
    another operation x20 -> x0, other arithmetic: 92 us -> none  [the longest x12 49.7 us: compress(): factor = jnp.linalg.cholesky(metric)]
    slice x11 -> x0, local copies, waits for them, and re-layouts: 82.1 us -> none  [the longest x2 36.8 us: body(): once_more = apply_band(factor_deep, blocked[1:-1])]
    unnamed x32 -> x0, local copies, waits for them, and re-layouts: 66.7 us -> none
    dot_general x17 -> x0, matrix products: 55.6 us -> none  [the longest x3 31.5 us: apply_band(): jnp.einsum('cbj,brj->cbr', windows, blocked, precision=lax.Precision.HIGH...]
    scatter x1 -> x0, local copies, waits for them, and re-layouts: 17.8 us -> none  [band_blocks(): return blocked.at[:, row_index, columns].set(values)]
    ppermute x4 -> x0, starting transfers between devices: 10.1 us -> none  [the longest x2 7.55 us: padded(): lax.ppermute(lax.slice_in_dim(block, block.shape[dim] - width, None, axis...]
  transfers between devices with their start and end apart: 6 -> 0, of which waited for: 2 -> 0; matrix products, arithmetic and copies ran while one was open for 15% -> 0% of each run, Pallas kernels for 0% -> 0%
where the time goes in v1:
time: 147 us
  Pallas kernels  145 us (99%)
    pallas_call x1, Pallas kernels, make_second(): pl.pallas_call(functools.partial(second_kernel, total), out_shape=[shape(...  47.9 us
    pallas_call x2, Pallas kernels, all_total(): pl.pallas_call(functools.partial(total_kernel, n, owners), out_shape=jax....  32.3 us
    pallas_call x1, Pallas kernels, make_last(): pl.pallas_call(functools.partial(last_kernel, total), out_shape=jax.Shape...  30 us
    pallas_call x1, Pallas kernels, make_first(): pl.pallas_call(first_kernel, out_shape=[jax.ShapeDtypeStruct((2 * width,...  23.2 us
    pallas_call x1, Pallas kernels, halos(): pl.pallas_call(functools.partial(halo_kernel, n), out_shape=[jax.ShapeDty...  11.9 us

profile of v1, /device:TPU:0, one launch (start us, length us, event | category | flops | bytes accessed | tf_op | source)
XLA Modules:
  0.0 146.7 jit_solution(11625039434685935057)
XLA Ops:
  0.0 1.4 copy.4.offsets
  1.4 11.9 %shard_map.37 = (f32[64,384]{1,0:T(8,128)}, f32[64,384]{1,0:T(8,128)}, f32[128,256]{1,0:T(8,128)}, f32[128,256]{1,0:T(8,128)}) custom-call(f32[64,4096]{1,0:T(8,128)} %source.3, f32[128,4096]{1,0:T(8,128)} %band.3), custom_call_target="tpu_custom_call" | custom-call | tf_op jit(solution)/shard_map/pallas_call | solution.py:75
  13.3 23.2 %shard_map.38 = (f32[128,4608]{1,0:T(8,128)}, bf16[36,128,384]{2,1,0:T(8,128)(2,1)}, bf16[36,128,384]{2,1,0:T(8,128)(2,1)}, f32[128,128]{1,0:T(8,128)}) custom-call(f32[64,4096]{1,0:T(8,128)} %source.3, f32[128,4096]{1,0:T(8,128)} %band.3, s32[128,1]{1,0:T(8,128)} %copy.4.offsets, f32[64,384]{1,0:T(8,128)} %get-tuple-element.17.low_s, ...), custom_call_target="tpu_custom_call" | custom-call | tf_op jit(solution)/shard_map/pallas_call | solution.py:274
  36.5 16.9 %shard_map.39 = f32[16,8,128]{2,1,0:T(8,128)} custom-call(f32[16,8,128]{2,1,0:T(8,128)} %bitcast.8), custom_call_target="tpu_custom_call" | custom-call | tf_op jit(solution)/shard_map/pallas_call | solution.py:197
  53.4 47.9 %shard_map.40 = (f32[128,4096]{1,0:T(8,128)}, f32[128,4096]{1,0:T(8,128)}, f32[128,128]{1,0:T(8,128)}, f32[256,128]{1,0:T(8,128)}) custom-call(f32[128,128]{1,0:T(8,128)} %bitcast.6, f32[128,4608]{1,0:T(8,128)} %get-tuple-element.22.first, bf16[36,128,384]{2,1,0:T(8,128)(2,1)} %get-tuple-element.23.upper, bf16[36,128,384]{2,1,0:T(8,128)(2,1)} %get-tuple-element.24.lower), custom_call_target="tpu_custom_call" | custom-call | tf_op jit(solution)/shard_map/pallas_call | solution.py:376
  101.4 15.3 %shard_map.41 = f32[32,8,128]{2,1,0:T(8,128)} custom-call(f32[32,8,128]{2,1,0:T(8,128)} %bitcast.7), custom_call_target="tpu_custom_call" | custom-call | tf_op jit(solution)/shard_map/pallas_call | solution.py:197
  116.7 30.0 %shard_map.42 = f32[128,4096]{1,0:T(8,128)} custom-call(f32[256,128]{1,0:T(8,128)} %bitcast.5, f32[128,128]{1,0:T(8,128)} %get-tuple-element.26.corner, f32[128,4096]{1,0:T(8,128)} %get-tuple-element.27.factor, f32[128,4096]{1,0:T(8,128)} %get-tuple-element.28.squared), custom_call_target="tpu_custom_call" | custom-call | tf_op jit(solution)/shard_map/pallas_call | solution.py:415

commit v2 on v1

--- a/solution.py
+++ b/solution.py
@@ -10,9 +10,10 @@
 HB = 128
 K2 = 128
 SUB = 8
+LANE = 128
 MESH = pl.DeviceIdType.MESH
 VMEM = pl.BlockSpec(memory_space=pltpu.VMEM)
-ANY = pl.BlockSpec(memory_space=pl.ANY)
+HBM = pl.BlockSpec(memory_space=pltpu.HBM)
 NT = (((1,), (1,)), ((), ()))
 
 
@@ -75,11 +76,13 @@
     return pl.pallas_call(
         functools.partial(halo_kernel, n),
         out_shape=[jax.ShapeDtypeStruct(shape, jnp.float32) for shape in shapes],
-        in_specs=[ANY] * 2,
+        in_specs=[HBM] * 2,
         out_specs=[VMEM] * 4,
         scratch_shapes=[pltpu.VMEM(shape, jnp.float32) for shape in shapes]
         + [pltpu.SemaphoreType.DMA((4,)), pltpu.SemaphoreType.DMA((4,))],
-        compiler_params=pltpu.CompilerParams(collective_id=0, has_side_effects=True),
+        compiler_params=pltpu.CompilerParams(
+            collective_id=0, has_side_effects=True, vmem_limit_bytes=8 << 20
+        ),
     )(source, band)
 
 
@@ -208,7 +211,9 @@
             dma((n,)),
             dma((owners,)),
         ],
-        compiler_params=pltpu.CompilerParams(collective_id=ident, has_side_effects=True),
+        compiler_params=pltpu.CompilerParams(
+            collective_id=ident, has_side_effects=True, vmem_limit_bytes=8 << 20
+        ),
     )(value.reshape(shape))
     return summed.reshape(rows, columns)
 
@@ -286,40 +291,72 @@
             pltpu.VMEM((width, deep + 2 * HB), jnp.bfloat16),
             pltpu.VMEM((diagonals, deep), jnp.float32),
         ],
-        compiler_params=pltpu.CompilerParams(vmem_limit_bytes=60 << 20),
+        compiler_params=pltpu.CompilerParams(vmem_limit_bytes=28 << 20),
     )(source, band, offsets.reshape(diagonals, 1), *edges)
 
 
+def splat(value):
+    return jnp.broadcast_to(value, (SUB, LANE))
+
+
 def eliminate(metric, right):
-    order = metric.shape[0]
-    tiles = order // SUB
-    s = [metric[SUB * t : SUB * t + SUB] for t in range(tiles)]
-    y = [right[SUB * t : SUB * t + SUB] for t in range(tiles)]
-    rows = lax.broadcasted_iota(jnp.int32, (SUB, 1), 0)
-    for j in range(order):
-        t0, r = divmod(j, SUB)
-        scale = lax.rsqrt(s[t0][r : r + 1, j : j + 1])
-        pivot_s = s[t0][r : r + 1] * scale
-        pivot_y = y[t0][r : r + 1] * scale
-        for t in range(t0, tiles):
-            column = s[t][:, j : j + 1] * scale
-            if t == t0:
-                column = jnp.where(rows > r, column, 0.0)
-                y[t] = jnp.where(rows == r, pivot_y, y[t])
-            s[t] = s[t] - column * pivot_s
-            y[t] = y[t] - column * pivot_y
-    return jnp.concatenate(y, axis=0)
+    tiles = metric.shape[0] // SUB
+    part = [slice(SUB * t, SUB * t + SUB) for t in range(tiles)]
+    state = [[metric[part[t]], right[part[t]]] for t in range(tiles)]
+    rows = lax.broadcasted_iota(jnp.int32, (SUB, LANE), 0)
+    solved = []
+    steps = range(SUB)
+    for t0 in range(tiles):
+        at = SUB * t0
+        core = {
+            (i, k): splat(state[t0][0][i : i + 1, at + k : at + k + 1])
+            for i in steps
+            for k in range(i, SUB)
+        }
+        pivots = [[splat(half[i : i + 1]) for half in state[t0]] for i in steps]
+        inverse = []
+        for i in steps:
+            inverse.append(1.0 / core[i, i])
+            for k in range(i + 1, SUB):
+                ratio = core[i, k] * inverse[i]
+                for m in range(k, SUB):
+                    core[k, m] = core[k, m] - ratio * core[i, m]
+                pivots[k] = [p - ratio * q for p, q in zip(pivots[k], pivots[i])]
+        result = jnp.zeros((SUB, LANE), jnp.float32)
+        for i in steps:
+            result = jnp.where(rows == i, pivots[i][1] * lax.rsqrt(core[i, i]), result)
+        solved.append(result)
+        for t in range(t0 + 1, tiles):
+            scaled = []
+            for k in steps:
+                column = splat(state[t][0][:, at + k : at + k + 1])
+                for i in range(k):
+                    column = column - scaled[i] * core[i, k]
+                scaled.append(column * inverse[k])
+            for half in range(2):
+                value = state[t][half]
+                for k in steps:
+                    value = value - scaled[k] * pivots[k][half]
+                state[t][half] = value
+    return jnp.concatenate(solved, axis=0)
 
 
 def compress(grammian, retain):
     spanning = grammian[:retain]
+    wide = spanning.shape[1] > retain
+    across = lax.broadcasted_iota(jnp.int32, (retain, retain), 1)
+    down = lax.broadcasted_iota(jnp.int32, (retain, retain), 0)
+    unit = jnp.where(across == down, 1.0, 0.0)
     coeffs = None
     for repeat in range(2):
         if repeat > 0:
             spanning = exact(coeffs, grammian)
         metric = exact(exact(spanning, grammian), spanning, NT)
         metric = 0.5 * (metric + metric.T)
-        coeffs = eliminate(metric, spanning)
+        if wide:
+            coeffs = exact(eliminate(metric, unit), spanning)
+        else:
+            coeffs = eliminate(metric, spanning)
     return coeffs
 
 
@@ -389,7 +426,7 @@
             pltpu.VMEM((keep, deep - 2 * HB), jnp.bfloat16),
             pltpu.VMEM((keep, deep - 2 * HB), jnp.bfloat16),
         ],
-        compiler_params=pltpu.CompilerParams(vmem_limit_bytes=60 << 20),
+        compiler_params=pltpu.CompilerParams(vmem_limit_bytes=28 << 20),
     )(summed, first, upper, lower)
 
 
@@ -417,7 +454,7 @@
         out_shape=jax.ShapeDtypeStruct((K2, factor.shape[1]), jnp.float32),
         in_specs=[VMEM] * 4,
         out_specs=VMEM,
-        compiler_params=pltpu.CompilerParams(vmem_limit_bytes=60 << 20),
+        compiler_params=pltpu.CompilerParams(vmem_limit_bytes=28 << 20),
     )(summed, corner, factor, squared)
 
 

time: 147 us -> 111 us (0.76)
  Pallas kernels: 145 us -> 107 us
  local copies, waits for them, and re-layouts: 1.39 us -> 3.58 us
    pallas_call x1, Pallas kernels: 47.9 us -> 30.9 us  [make_second(): pl.pallas_call(functools.partial(second_kernel, total), out_shape=[shape(...]
    pallas_call x1, Pallas kernels: 30 us -> 16.1 us  [make_last(): pl.pallas_call(functools.partial(last_kernel, total), out_shape=jax.Shape...]
    pallas_call x1, Pallas kernels: 23.2 us -> 19.7 us  [make_first(): pl.pallas_call(first_kernel, out_shape=[jax.ShapeDtypeStruct((2 * width,...]
    pallas_call x2, Pallas kernels: 32.3 us -> 29.3 us  [all_total(): pl.pallas_call(functools.partial(total_kernel, n, owners), out_shape=jax....]
    unnamed x0 -> x8, local copies, waits for them, and re-layouts: none -> 2.82 us
where the time goes in v2:
time: 111 us
  Pallas kernels  107 us (96%)
  local copies, waits for them, and re-layouts  3.58 us (3%)
    pallas_call x1, Pallas kernels, make_second(): pl.pallas_call(functools.partial(second_kernel, total), out_shape=[shape(...  30.9 us
    pallas_call x2, Pallas kernels, all_total(): pl.pallas_call(functools.partial(total_kernel, n, owners), out_shape=jax....  29.3 us
    pallas_call x1, Pallas kernels, make_first(): pl.pallas_call(first_kernel, out_shape=[jax.ShapeDtypeStruct((2 * width,...  19.7 us
    pallas_call x1, Pallas kernels, make_last(): pl.pallas_call(functools.partial(last_kernel, total), out_shape=jax.Shape...  16.1 us
    pallas_call x1, Pallas kernels, halos(): pl.pallas_call(functools.partial(halo_kernel, n), out_shape=[jax.ShapeDty...  10.9 us
    unnamed x8, local copies, waits for them, and re-layouts  2.82 us

profile of v2, /device:TPU:0, one launch (start us, length us, event | category | flops | bytes accessed | tf_op | source)
XLA Modules:
  0.0 110.6 jit_solution(3590951461923441604)
XLA Ops:
  0.0 0.8 copy.4.offsets
  0.8 0.0 copy-start
  0.8 1.6 %copy-done = f32[128,4096]{1,0:T(8,128)S(1)} copy-done((f32[128,4096]{1,0:T(8,128)S(1)}, f32[128,4096]{1,0:T(8,128)}, u32[]{:S(2)}) %copy-start) | copy-done | bytes 2097176
  2.4 0.0 copy-start.2
  2.4 1.2 %copy-done.2 = f32[64,4096]{1,0:T(8,128)S(1)} copy-done((f32[64,4096]{1,0:T(8,128)S(1)}, f32[64,4096]{1,0:T(8,128)}, u32[]{:S(2)}) %copy-start.2) | copy-done | bytes 1048600
  3.6 0.0 copy-start.1
  3.6 0.0 copy-start.3
  3.6 10.9 %shard_map.37 = (f32[64,384]{1,0:T(8,128)S(1)}, f32[64,384]{1,0:T(8,128)S(1)}, f32[128,256]{1,0:T(8,128)S(1)}, f32[128,256]{1,0:T(8,128)S(1)}) custom-call(f32[64,4096]{1,0:T(8,128)S(1)} %copy-done.2, f32[128,4096]{1,0:T(8,128)S(1)} %copy-done), custom_call_target="tpu_custom_call" | custom-call | tf_op jit(solution)/shard_map/pallas_call | solution.py:76
  14.5 0.0 copy-done.1
  14.5 0.0 copy-done.3
  14.5 19.7 %shard_map.38 = (f32[128,4608]{1,0:T(8,128)S(1)}, bf16[36,128,384]{2,1,0:T(8,128)(2,1)S(1)}, bf16[36,128,384]{2,1,0:T(8,128)(2,1)S(1)}, f32[128,128]{1,0:T(8,128)S(1)}) custom-call(f32[64,4096]{1,0:T(8,128)S(1)} %copy-done.3, f32[128,4096]{1,0:T(8,128)S(1)} %copy-done.1, s32[128,1]{1,0:T(8,128)S(1)} %copy.4.offsets, f32[64,384]{1,0:T(8,128)S(1)} %get-tuple-element.17.low_s, ...), custom_call_target="tpu_custom_call" | custom-call | tf_op jit(solution)/shard_map/pallas_call | solution.py:279
  34.2 15.3 %shard_map.39 = f32[16,8,128]{2,1,0:T(8,128)S(1)} custom-call(f32[16,8,128]{2,1,0:T(8,128)S(1)} %bitcast.8), custom_call_target="tpu_custom_call" | custom-call | tf_op jit(solution)/shard_map/pallas_call | solution.py:200
  49.5 30.9 %shard_map.40 = (f32[128,4096]{1,0:T(8,128)S(1)}, f32[128,4096]{1,0:T(8,128)S(1)}, f32[128,128]{1,0:T(8,128)S(1)}, f32[256,128]{1,0:T(8,128)S(1)}) custom-call(f32[128,128]{1,0:T(8,128)S(1)} %bitcast.6, f32[128,4608]{1,0:T(8,128)S(1)} %get-tuple-element.22.first, bf16[36,128,384]{2,1,0:T(8,128)(2,1)S(1)} %get-tuple-element.23.upper, ...), custom_call_target="tpu_custom_call" | custom-call | tf_op jit(solution)/shard_map/pallas_call | solution.py:413
  80.4 14.0 %shard_map.41 = f32[32,8,128]{2,1,0:T(8,128)S(1)} custom-call(f32[32,8,128]{2,1,0:T(8,128)S(1)} %bitcast.7), custom_call_target="tpu_custom_call" | custom-call | tf_op jit(solution)/shard_map/pallas_call | solution.py:200
  94.5 16.1 %shard_map.42 = f32[128,4096]{1,0:T(8,128)} custom-call(f32[256,128]{1,0:T(8,128)S(1)} %bitcast.5, f32[128,128]{1,0:T(8,128)S(1)} %get-tuple-element.26.corner, f32[128,4096]{1,0:T(8,128)S(1)} %get-tuple-element.27.factor, f32[128,4096]{1,0:T(8,128)S(1)} %get-tuple-element.28.squared), custom_call_target="tpu_custom_call" | custom-call | tf_op jit(solution)/shard_map/pallas_call | solution.py:452
Async XLA Ops:
  0.8 1.6 %copy-start = (f32[128,4096]{1,0:T(8,128)S(1)}, f32[128,4096]{1,0:T(8,128)}, u32[]{:S(2)}) copy-start(f32[128,4096]{1,0:T(8,128)} %band.3) | copy-start | bytes 6291460
  2.4 1.2 %copy-start.2 = (f32[64,4096]{1,0:T(8,128)S(1)}, f32[64,4096]{1,0:T(8,128)}, u32[]{:S(2)}) copy-start(f32[64,4096]{1,0:T(8,128)} %source.3) | copy-start | bytes 3145732
  3.6 10.9 %copy-start.1 = (f32[128,4096]{1,0:T(8,128)S(1)}, f32[128,4096]{1,0:T(8,128)}, u32[]{:S(2)}) copy-start(f32[128,4096]{1,0:T(8,128)} %band.3) | copy-start | bytes 6291460
  3.6 10.9 %copy-start.3 = (f32[64,4096]{1,0:T(8,128)S(1)}, f32[64,4096]{1,0:T(8,128)}, u32[]{:S(2)}) copy-start(f32[64,4096]{1,0:T(8,128)} %source.3) | copy-start | bytes 3145732

commit v3 on v2

--- a/solution.py
+++ b/solution.py
@@ -226,6 +226,11 @@
     )
 
 
+def squares(high, low):
+    mixed = bf(high, low, NT)
+    return bf(high, high, NT) + mixed + mixed.T
+
+
 def columns_of(block, count=1):
     return pl.ds(pl.multiple_of(block * HB, HB), count * HB)
 
@@ -266,9 +271,9 @@
         )
         return 0
 
-    lax.fori_loop(0, blocks, step, 0, unroll=2)
+    lax.fori_loop(0, blocks, step, 0, unroll=4)
     inner = first[:, pl.ds(2 * HB, local)]
-    gram[...] = exact(inner, inner, NT)
+    gram[...] = squares(*halves(inner))
 
 
 def make_first(source, band, offsets, edges):
@@ -390,7 +395,7 @@
         once_low[:, columns_of(block)] = bottom
         return 0
 
-    lax.fori_loop(0, blocks - 2, once, 0, unroll=2)
+    lax.fori_loop(0, blocks - 2, once, 0, unroll=4)
 
     def twice(block, _):
         window = columns_of(block, 3)
@@ -399,11 +404,12 @@
         )
         return 0
 
-    lax.fori_loop(0, blocks - 4, twice, 0, unroll=2)
+    lax.fori_loop(0, blocks - 4, twice, 0, unroll=4)
     middle = pl.ds(2 * HB, local)
     factor[...] = high[:, middle].astype(jnp.float32) + low[:, middle].astype(jnp.float32)
-    gram[:keep] = exact(factor[...], squared[...], NT)
-    gram[keep:] = exact(squared[...], squared[...], NT)
+    top, bottom = halves(squared[...])
+    gram[:keep] = banded(high[:, middle], low[:, middle], top, bottom)
+    gram[keep:] = squares(top, bottom)
 
 
 def make_second(summed, first, upper, lower, total):

time: 111 us -> 104 us (0.937)
  Pallas kernels: 107 us -> 101 us
    pallas_call x1, Pallas kernels: 30.9 us -> 26.9 us  [make_second(): pl.pallas_call(functools.partial(second_kernel, total), out_shape=[shape(...]
    pallas_call x1, Pallas kernels: 19.7 us -> 17 us  [make_first(): pl.pallas_call(first_kernel, out_shape=[jax.ShapeDtypeStruct((2 * width,...]
where the time goes in v3:
time: 104 us
  Pallas kernels  101 us (97%)
  local copies, waits for them, and re-layouts  3.58 us (3%)
    pallas_call x2, Pallas kernels, all_total(): pl.pallas_call(functools.partial(total_kernel, n, owners), out_shape=jax....  29.7 us
    pallas_call x1, Pallas kernels, make_second(): pl.pallas_call(functools.partial(second_kernel, total), out_shape=[shape(...  26.9 us
    pallas_call x1, Pallas kernels, make_first(): pl.pallas_call(first_kernel, out_shape=[jax.ShapeDtypeStruct((2 * width,...  17 us
    pallas_call x1, Pallas kernels, make_last(): pl.pallas_call(functools.partial(last_kernel, total), out_shape=jax.Shape...  16.1 us
    pallas_call x1, Pallas kernels, halos(): pl.pallas_call(functools.partial(halo_kernel, n), out_shape=[jax.ShapeDty...  10.9 us
    unnamed x8, local copies, waits for them, and re-layouts  2.82 us

profile of v3, /device:TPU:0, one launch (start us, length us, event | category | flops | bytes accessed | tf_op | source)
XLA Modules:
  0.0 104.3 jit_solution(16007661212151630450)
XLA Ops:
  0.0 0.8 copy.4.offsets
  0.8 0.0 copy-start
  0.8 1.6 %copy-done = f32[128,4096]{1,0:T(8,128)S(1)} copy-done((f32[128,4096]{1,0:T(8,128)S(1)}, f32[128,4096]{1,0:T(8,128)}, u32[]{:S(2)}) %copy-start) | copy-done | bytes 2097176
  2.4 0.0 copy-start.2
  2.4 1.2 %copy-done.2 = f32[64,4096]{1,0:T(8,128)S(1)} copy-done((f32[64,4096]{1,0:T(8,128)S(1)}, f32[64,4096]{1,0:T(8,128)}, u32[]{:S(2)}) %copy-start.2) | copy-done | bytes 1048600
  3.6 0.0 copy-start.1
  3.6 0.0 copy-start.3
  3.6 10.9 %shard_map.37 = (f32[64,384]{1,0:T(8,128)S(1)}, f32[64,384]{1,0:T(8,128)S(1)}, f32[128,256]{1,0:T(8,128)S(1)}, f32[128,256]{1,0:T(8,128)S(1)}) custom-call(f32[64,4096]{1,0:T(8,128)S(1)} %copy-done.2, f32[128,4096]{1,0:T(8,128)S(1)} %copy-done), custom_call_target="tpu_custom_call" | custom-call | tf_op jit(solution)/shard_map/pallas_call | solution.py:76
  14.5 0.0 copy-done.1
  14.5 0.0 copy-done.3
  14.5 17.0 %shard_map.38 = (f32[128,4608]{1,0:T(8,128)S(1)}, bf16[36,128,384]{2,1,0:T(8,128)(2,1)S(1)}, bf16[36,128,384]{2,1,0:T(8,128)(2,1)S(1)}, f32[128,128]{1,0:T(8,128)S(1)}) custom-call(f32[64,4096]{1,0:T(8,128)S(1)} %copy-done.3, f32[128,4096]{1,0:T(8,128)S(1)} %copy-done.1, s32[128,1]{1,0:T(8,128)S(1)} %copy.4.offsets, f32[64,384]{1,0:T(8,128)S(1)} %get-tuple-element.17.low_s, ...), custom_call_target="tpu_custom_call" | custom-call | tf_op jit(solution)/shard_map/pallas_call | solution.py:284
  31.5 15.5 %shard_map.39 = f32[16,8,128]{2,1,0:T(8,128)S(1)} custom-call(f32[16,8,128]{2,1,0:T(8,128)S(1)} %bitcast.8), custom_call_target="tpu_custom_call" | custom-call | tf_op jit(solution)/shard_map/pallas_call | solution.py:200
  47.0 26.9 %shard_map.40 = (f32[128,4096]{1,0:T(8,128)S(1)}, f32[128,4096]{1,0:T(8,128)S(1)}, f32[128,128]{1,0:T(8,128)S(1)}, f32[256,128]{1,0:T(8,128)S(1)}) custom-call(f32[128,128]{1,0:T(8,128)S(1)} %bitcast.6, f32[128,4608]{1,0:T(8,128)S(1)} %get-tuple-element.22.first, bf16[36,128,384]{2,1,0:T(8,128)(2,1)S(1)} %get-tuple-element.23.upper, ...), custom_call_target="tpu_custom_call" | custom-call | tf_op jit(solution)/shard_map/pallas_call | solution.py:419
  73.9 14.2 %shard_map.41 = f32[32,8,128]{2,1,0:T(8,128)S(1)} custom-call(f32[32,8,128]{2,1,0:T(8,128)S(1)} %bitcast.7), custom_call_target="tpu_custom_call" | custom-call | tf_op jit(solution)/shard_map/pallas_call | solution.py:200
  88.2 16.1 %shard_map.42 = f32[128,4096]{1,0:T(8,128)} custom-call(f32[256,128]{1,0:T(8,128)S(1)} %bitcast.5, f32[128,128]{1,0:T(8,128)S(1)} %get-tuple-element.26.corner, f32[128,4096]{1,0:T(8,128)S(1)} %get-tuple-element.27.factor, f32[128,4096]{1,0:T(8,128)S(1)} %get-tuple-element.28.squared), custom_call_target="tpu_custom_call" | custom-call | tf_op jit(solution)/shard_map/pallas_call | solution.py:458
Async XLA Ops:
  0.8 1.6 %copy-start = (f32[128,4096]{1,0:T(8,128)S(1)}, f32[128,4096]{1,0:T(8,128)}, u32[]{:S(2)}) copy-start(f32[128,4096]{1,0:T(8,128)} %band.3) | copy-start | bytes 6291460
  2.4 1.2 %copy-start.2 = (f32[64,4096]{1,0:T(8,128)S(1)}, f32[64,4096]{1,0:T(8,128)}, u32[]{:S(2)}) copy-start(f32[64,4096]{1,0:T(8,128)} %source.3) | copy-start | bytes 3145732
  3.6 10.9 %copy-start.1 = (f32[128,4096]{1,0:T(8,128)S(1)}, f32[128,4096]{1,0:T(8,128)}, u32[]{:S(2)}) copy-start(f32[128,4096]{1,0:T(8,128)} %band.3) | copy-start | bytes 6291460
  3.6 10.9 %copy-start.3 = (f32[64,4096]{1,0:T(8,128)S(1)}, f32[64,4096]{1,0:T(8,128)}, u32[]{:S(2)}) copy-start(f32[64,4096]{1,0:T(8,128)} %source.3) | copy-start | bytes 3145732
